TPU v7x, 32 devices: a whole 2x2x4 slice. The times are simulated.
32 devices in a mesh: tm: 16 (over z, y, x), rows: 2 (over core).
Axes of the slice: x: 2, y: 2, z: 4, core: 2. Of those that a mesh axis runs over, the one named last changes fastest.
Arguments:
- resid: float32 [2, 16, 16, 512], P(None, 'tm', 'rows'), may hold values from -3 to 3
- basis: float32 [4, 2, 16, 16, 512], P(None, None, 'tm', 'rows'), may hold values from -0.01171875 to 0.01171875
Outputs:
- precond: float32 [2, 16, 16, 512], P(None, 'tm', 'rows')
- image: float32 [2, 16, 16, 512], P(None, 'tm', 'rows')
- gram: float32 [5], replicated
All inputs are finite; a program needn't handle non-finite values.
Results may differ from a plain program's by a relative error of at most 0.0005.
Values sent between devices are 32-bit elements; how exact they have to be, the bound alone decides.
A program may use at most 64 MiB of HBM per device.

v0:
```python
import math
import jax
import jax.numpy as jnp
from jax import lax
from jax.sharding import PartitionSpec as P

SWEEPS = 4
ALPHA = 0.01


def padded_2(shard, sides, width):
    for axis, dim in sides:
        count, length = (lax.axis_size(axis), shard.shape[dim])
        up = [(i, (i + 1) % count) for i in range(count - 1)]
        down = [(j, i) for i, j in up]
        last = lax.slice_in_dim(shard, length - width, length, axis=dim)
        first = lax.slice_in_dim(shard, 0, width, axis=dim)
        before = lax.ppermute(last, axis, up)
        after = lax.ppermute(first, axis, down)
        shard = jnp.concatenate([before, shard, after], axis=dim)
    return shard


def shifted(value, axis, steps):
    count = lax.axis_size(axis)
    first, last = (max(0, -steps), min(count, count - steps))
    return lax.ppermute(value, axis, [(source, source + steps) for source in range(first, last)])


def neighbours(padded):
    middle = padded[:, 1:-1]
    sides = jnp.pad(middle, ((0, 0), (0, 0), (1, 1)))
    return padded[:, 2:] + padded[:, :-2] + sides[:, :, 2:] + sides[:, :, :-2]


def cmul(left, right_re, right_im):
    return jnp.stack(
        [left[0] * right_re - left[1] * right_im, left[0] * right_im + left[1] * right_re]
    )


def phases(first, second, steps):
    turns = first * second % steps
    angle = turns.astype(jnp.float32) * (2.0 * math.pi / steps)
    return (jnp.cos(angle), jnp.sin(angle))


def on_device(resid, basis):
    steps = lax.axis_size("tm")
    coupling = 16.0 / (steps * steps)
    me = lax.axis_index("tm")
    rows_dev = resid.shape[2]
    cols = resid.shape[3]
    cells = rows_dev * cols
    piece = cells // steps
    mine = me.astype(jnp.float32)
    gamma = jnp.power(jnp.float32(ALPHA), mine / steps)
    scaled = resid[:, 0] * gamma
    ordinal = jnp.arange(steps, dtype=jnp.int32)
    cos_table, sin_table = phases(ordinal[:, None], ordinal[None, :], steps)
    blocks = lax.all_to_all(
        scaled.reshape(1, 2, cells), "tm", split_axis=2, concat_axis=0, tiled=True
    )
    flat = blocks.reshape(steps, 2 * piece)
    real_part = jnp.dot(cos_table, flat, precision=lax.Precision.HIGHEST)
    imag_part = -jnp.dot(sin_table, flat, precision=lax.Precision.HIGHEST)
    stacked = jnp.stack([real_part, imag_part], 1).reshape(steps, 2, 2, piece)
    spectrum = lax.all_to_all(stacked, "tm", split_axis=0, concat_axis=3, tiled=True)
    rhat = spectrum[0].reshape(2, 2, rows_dev, cols)
    base = jnp.power(jnp.float32(ALPHA), jnp.float32(1.0) / steps)
    angle = mine * (2.0 * math.pi / steps)
    lam_re = 1.0 - base * jnp.cos(angle)
    lam_im = base * jnp.sin(angle)
    disp_spec = rhat[:, 0]
    right = cmul(disp_spec, lam_re, lam_im) + rhat[:, 1]
    den_re = lam_re * lam_re - lam_im * lam_im + 4.0 * coupling
    den_im = 2.0 * lam_re * lam_im
    magnitude = den_re * den_re + den_im * den_im
    inv_re = den_re / magnitude
    inv_im = -den_im / magnitude
    uhat = cmul(right, inv_re, inv_im)
    for sweep in range(SWEEPS - 1):
        padded = padded_2(uhat, (("rows", 1),), 1)
        uhat = cmul(right + coupling * neighbours(padded), inv_re, inv_im)
    vhat = cmul(uhat, lam_re, lam_im) - disp_spec
    yhat = jnp.stack([uhat, vhat], 1)
    spread = lax.all_to_all(
        yhat.reshape(1, 2, 2, cells), "tm", split_axis=3, concat_axis=0, tiled=True
    )
    real_rows = spread[:, 0].reshape(steps, 2 * piece)
    imag_rows = spread[:, 1].reshape(steps, 2 * piece)
    undo = jnp.power(jnp.float32(ALPHA), -ordinal.astype(jnp.float32) / steps) / steps
    history = jnp.dot(cos_table, real_rows, precision=lax.Precision.HIGHEST) - jnp.dot(
        sin_table, imag_rows, precision=lax.Precision.HIGHEST
    )
    history = (history * undo[:, None]).reshape(steps, 2, piece)
    returned = lax.all_to_all(history, "tm", split_axis=0, concat_axis=2, tiled=True)
    precond = returned[0].reshape(2, rows_dev, cols)
    earlier = shifted(precond, "tm", 1)
    disp_rim = padded_2(precond[0:1], (("rows", 1),), 1)
    laplace = neighbours(disp_rim)[0] - 4.0 * precond[0]
    first = precond[0] - earlier[0] - precond[1]
    second = precond[1] - earlier[1] - coupling * laplace
    image = jnp.stack([first, second])
    inner = jnp.sum(basis[:, :, 0] * image[None], axis=(1, 2, 3))
    count = 2.0 * steps * rows_dev * lax.axis_size("rows") * cols
    squares = jnp.sum(image * image) / count
    local_terms = jnp.concatenate([inner, squares[None]])
    gram = lax.psum(local_terms, ("tm", "rows"))
    return (precond[:, None], image[:, None], gram)


def solution(mesh):
    in_specs = (P(None, "tm", "rows", None), P(None, None, "tm", "rows", None))
    out_specs = (P(None, "tm", "rows", None), P(None, "tm", "rows", None), P())
    return jax.shard_map(
        on_device, mesh=mesh, in_specs=in_specs, out_specs=out_specs, check_vma=False
    )
```

profile of v0, /device:TPU:0, one launch (start us, length us, event | category | flops | bytes accessed | tf_op | source)
XLA Modules:
  0.0 169.4 jit_solution(10434036143663607024)
XLA Ops:
  0.7 0.8 broadcast_multiply_fusion
  1.4 0.6 copy.44
  2.1 0.5 broadcast.139
  2.6 19.4 %reduce.4 = f32[4096,2]{1,0:T(8,128)} reduce(f32[4096,1,2]{2,1,0:T(1,128)S(1)} %bitcast.83, f32[]{:T(128)} %broadcast.139), dimensions={1}, to_apply=%bitcast.65.reduce_sub_computation | reduce | bytes 65540
  22.0 3.0 %reshape.138 = f32[16,1,512]{2,1,0:T(1,128)S(1)} reshape(f32[4096,2]{1,0:T(8,128)} %reduce.4) | data formatting | bytes 65536
  25.0 15.5 %all_to_all.63 = f32[16,1,512]{2,1,0:T(1,128)S(1)} all-to-all(f32[16,1,512]{2,1,0:T(1,128)S(1)} %reshape.138), channel_id=1, replica_groups=mesh['tm'=16,'rows'=2] {'tm'}, dimensions={0} | all-to-all | bytes 65536 | tf_op jit(solution)/shard_map/all_to_all | solution.py:61
  40.5 0.7 reduce.5
  41.3 3.4 %reshape.139 = f32[4096,1,2]{2,1,0:T(1,128)S(1)} reshape(f32[16,512]{1,0:T(8,128)S(1)} %reduce.5) | data formatting | bytes 65536
  44.7 0.6 copy.45
  45.3 0.2 convolution_bitcast_fusion
  45.5 0.2 convolution_negate_fusion
  45.8 0.7 copy.48
  46.5 3.5 %all-to-all-start.1 = ((f32[16,2,2,256]{3,2,1,0:T(2,128)}), f32[16,2,2,256]{3,2,1,0:T(2,128)S(1)}, u32[]{:S(2)}, u32[]{:S(2)}) async-start(f32[16,2,2,256]{3,2,1,0:T(2,128)} %copy.48), calls=%async_computation.1 | async-start | bytes 131072 | tf_op jit(solution)/shard_map/all_to_all | solution.py:68
  50.2 7.2 %all-to-all-done.1 = f32[16,2,2,256]{3,2,1,0:T(2,128)S(1)} async-done(((f32[16,2,2,256]{3,2,1,0:T(2,128)}), f32[16,2,2,256]{3,2,1,0:T(2,128)S(1)}, u32[]{:S(2)}, u32[]{:S(2)}) %all-to-all-start.1) | async-done | bytes 65568 | tf_op jit(solution)/shard_map/all_to_all | solution.py:68
  57.6 1.3 collective-permute-start
  58.9 3.0 %collective-permute-start.1 = (f32[2,1,512]{2,1,0:T(1,128)S(1)}, f32[2,1,512]{2,1,0:T(1,128)S(1)}, u32[]{:S(2)}, u32[]{:S(2)}) collective-permute-start(f32[2,1,512]{2,1,0:T(1,128)S(1)} %get-tuple-element.26), channel_id=1, source_target_pairs={{0,1},{2,3},{4,5},{6,7},{8,9},{10,11},{12,13},{14,15},{16,17},{18,... | collective-permute-start | bytes 12296 | tf_op jit(solution)/shard_map/ppermute | solution.py:18
  62.0 0.8 collective-permute-done.1
  62.7 0.1 fusion.5
  62.9 1.3 collective-permute-start.2
  64.2 3.0 %collective-permute-start.3 = (f32[2,1,512]{2,1,0:T(1,128)S(1)}, f32[2,1,512]{2,1,0:T(1,128)S(1)}, u32[]{:S(2)}, u32[]{:S(2)}) collective-permute-start(f32[2,1,512]{2,1,0:T(1,128)S(1)} %get-tuple-element.22), channel_id=1, source_target_pairs={{0,1},{2,3},{4,5},{6,7},{8,9},{10,11},{12,13},{14,15},{16,17},{18,... | collective-permute-start | bytes 12296 | tf_op jit(solution)/shard_map/ppermute | solution.py:18
  67.2 0.0 collective-permute-done.2
  67.2 0.8 collective-permute-done.3
  68.0 0.1 fusion.9
  68.1 1.3 collective-permute-start.4
  69.4 3.2 %collective-permute-start.5 = (f32[2,1,512]{2,1,0:T(1,128)S(1)}, f32[2,1,512]{2,1,0:T(1,128)S(1)}, u32[]{:S(2)}, u32[]{:S(2)}) collective-permute-start(f32[2,1,512]{2,1,0:T(1,128)S(1)} %get-tuple-element.18), channel_id=1, source_target_pairs={{0,1},{2,3},{4,5},{6,7},{8,9},{10,11},{12,13},{14,15},{16,17},{18,... | collective-permute-start | bytes 12296 | tf_op jit(solution)/shard_map/ppermute | solution.py:18
  72.7 0.6 collective-permute-done.5
  73.3 0.1 fusion.13
  73.5 4.4 %copy.51 = f32[1,2,2,4096]{2,1,0,3:T(2,128)} copy(f32[1,2,2,4096]{3,1,2,0:T(2,128)S(1)} %pad_maximum_fusion.1) | data formatting | bytes 131072 | tf_op jit(solution)/shard_map/stack | solution.py:86
  77.9 8.1 %reshape.140 = f32[16,1,1024]{2,1,0:T(1,128)} reshape(f32[4096,1,2,2]{3,2,1,0:T(2,128)} %bitcast.81) | data formatting | bytes 131072
  86.0 3.5 %all-to-all-start.2 = ((f32[16,1,1024]{2,1,0:T(1,128)}), f32[16,1,1024]{2,1,0:T(1,128)S(1)}, u32[]{:S(2)}, u32[]{:S(2)}) async-start(f32[16,1,1024]{2,1,0:T(1,128)} %reshape.140), calls=%async_computation.2 | async-start | bytes 131072 | tf_op jit(solution)/shard_map/all_to_all | solution.py:87
  89.5 7.5 %all-to-all-done.2 = f32[16,1,1024]{2,1,0:T(1,128)S(1)} async-done(((f32[16,1,1024]{2,1,0:T(1,128)}), f32[16,1,1024]{2,1,0:T(1,128)S(1)}, u32[]{:S(2)}, u32[]{:S(2)}) %all-to-all-start.2) | async-done | bytes 65568 | tf_op jit(solution)/shard_map/all_to_all | solution.py:87
  97.0 0.8 reduce.6
  97.8 7.7 %reshape.141 = f32[4096,1,2,2]{3,2,1,0:T(2,128)} reshape(f32[16,1024]{1,0:T(8,128)S(1)} %reduce.6) | data formatting | bytes 131072
  105.6 3.6 %copy.57 = f32[1,2,2,16,256]{4,3,2,1,0:T(8,128)S(1)} copy(f32[1,2,2,16,256]{2,1,4,3,0:T(2,128)} %bitcast.82) | data formatting | bytes 131072 | tf_op jit(solution)/shard_map/all_to_all | solution.py:87
  109.2 0.2 fusion.42
  109.5 0.2 fusion
  109.7 10.0 %all_to_all.64 = f32[16,2,256]{2,1,0:T(2,128)S(1)} all-to-all(f32[16,2,256]{2,1,0:T(2,128)S(1)} %reshape.134), channel_id=1, replica_groups=mesh['tm'=16,'rows'=2] {'tm'}, dimensions={0} | all-to-all | bytes 65536 | tf_op jit(solution)/shard_map/all_to_all | solution.py:97
  119.7 0.1 slice_reduce_fusion
  119.8 2.6 %collective-permute-start.6 = (f32[2,8,512]{2,1,0:T(8,128)S(1)}, f32[2,8,512]{2,1,0:T(8,128)S(1)}, u32[]{:S(2)}, u32[]{:S(2)}) collective-permute-start(f32[2,8,512]{2,1,0:T(8,128)S(1)} %reshape_squeeze.15), channel_id=1, source_target_pairs={{0,2},{2,4},{4,6},{6,8},{8,10},{10,12},{12,14},{14,16},{16,18},{18... | collective-permute-start | bytes 98312 | tf_op jit(solution)/shard_map/ppermute | solution.py:27
  122.4 1.3 collective-permute-start.7
  123.7 3.0 %collective-permute-start.8 = (f32[1,1,512]{2,1,0:T(1,128)S(1)}, f32[1,1,512]{2,1,0:T(1,128)S(1)}, u32[]{:S(2)}, u32[]{:S(2)}) collective-permute-start(f32[1,1,512]{2,1,0:T(1,128)S(1)} %get-tuple-element.30), channel_id=1, source_target_pairs={{0,1},{2,3},{4,5},{6,7},{8,9},{10,11},{12,13},{14,15},{16,17},{18,... | collective-permute-start | bytes 6152 | tf_op jit(solution)/shard_map/ppermute | solution.py:18
  126.8 0.8 collective-permute-done.8
  127.6 0.1 fusion.26
  127.7 1.2 pad_maximum_fusion.18
  129.6 0.1 fusion.1
  129.7 0.1 pad_maximum_fusion.21
  129.8 0.6 broadcast_in_dim_reshape_squeeze.3
  130.4 39.0 %psum.7 = f32[5]{0:T(128)} all-reduce(f32[5]{0:T(128)S(1)} %pad_maximum_fusion.21), channel_id=1, replica_groups=mesh['tm'=16,'rows'=2] {'tm','rows'}, use_global_device_ids=true, to_apply=%region_2.3 | all-reduce | flops 5 | bytes 40 | tf_op jit(solution)/shard_map/psum | solution.py:109
  (42 shorter events, 0.5 us)
Async XLA Ops:
  46.5 11.0 %all-to-all-start.1 = ((f32[16,2,2,256]{3,2,1,0:T(2,128)}), f32[16,2,2,256]{3,2,1,0:T(2,128)S(1)}, u32[]{:S(2)}, u32[]{:S(2)}) async-start(f32[16,2,2,256]{3,2,1,0:T(2,128)} %copy.48), calls=%async_computation.1 | async-start | bytes 131072 | tf_op jit(solution)/shard_map/all_to_all | solution.py:68
  57.6 4.3 %collective-permute-start = (f32[2,1,512]{2,1,0:T(1,128)S(1)}, f32[2,1,512]{2,1,0:T(1,128)S(1)}, u32[]{:S(2)}, u32[]{:S(2)}) collective-permute-start(f32[2,1,512]{2,1,0:T(1,128)S(1)} %get-tuple-element.25), channel_id=1, source_target_pairs={{1,0},{3,2},{5,4},{7,6},{9,8},{11,10},{13,12},{15,14},{17,16},{19,... | collective-permute-start | bytes 12296 | tf_op jit(solution)/shard_map/ppermute | solution.py:19
  58.9 3.8 %collective-permute-start.1 = (f32[2,1,512]{2,1,0:T(1,128)S(1)}, f32[2,1,512]{2,1,0:T(1,128)S(1)}, u32[]{:S(2)}, u32[]{:S(2)}) collective-permute-start(f32[2,1,512]{2,1,0:T(1,128)S(1)} %get-tuple-element.26), channel_id=1, source_target_pairs={{0,1},{2,3},{4,5},{6,7},{8,9},{10,11},{12,13},{14,15},{16,17},{18,... | collective-permute-start | bytes 12296 | tf_op jit(solution)/shard_map/ppermute | solution.py:18
  62.9 4.3 %collective-permute-start.2 = (f32[2,1,512]{2,1,0:T(1,128)S(1)}, f32[2,1,512]{2,1,0:T(1,128)S(1)}, u32[]{:S(2)}, u32[]{:S(2)}) collective-permute-start(f32[2,1,512]{2,1,0:T(1,128)S(1)} %get-tuple-element.21), channel_id=1, source_target_pairs={{1,0},{3,2},{5,4},{7,6},{9,8},{11,10},{13,12},{15,14},{17,16},{19,... | collective-permute-start | bytes 12296 | tf_op jit(solution)/shard_map/ppermute | solution.py:19
  64.2 3.8 %collective-permute-start.3 = (f32[2,1,512]{2,1,0:T(1,128)S(1)}, f32[2,1,512]{2,1,0:T(1,128)S(1)}, u32[]{:S(2)}, u32[]{:S(2)}) collective-permute-start(f32[2,1,512]{2,1,0:T(1,128)S(1)} %get-tuple-element.22), channel_id=1, source_target_pairs={{0,1},{2,3},{4,5},{6,7},{8,9},{10,11},{12,13},{14,15},{16,17},{18,... | collective-permute-start | bytes 12296 | tf_op jit(solution)/shard_map/ppermute | solution.py:18
  68.1 4.5 %collective-permute-start.4 = (f32[2,1,512]{2,1,0:T(1,128)S(1)}, f32[2,1,512]{2,1,0:T(1,128)S(1)}, u32[]{:S(2)}, u32[]{:S(2)}) collective-permute-start(f32[2,1,512]{2,1,0:T(1,128)S(1)} %get-tuple-element.17), channel_id=1, source_target_pairs={{1,0},{3,2},{5,4},{7,6},{9,8},{11,10},{13,12},{15,14},{17,16},{19,... | collective-permute-start | bytes 12296 | tf_op jit(solution)/shard_map/ppermute | solution.py:19
  69.4 3.8 %collective-permute-start.5 = (f32[2,1,512]{2,1,0:T(1,128)S(1)}, f32[2,1,512]{2,1,0:T(1,128)S(1)}, u32[]{:S(2)}, u32[]{:S(2)}) collective-permute-start(f32[2,1,512]{2,1,0:T(1,128)S(1)} %get-tuple-element.18), channel_id=1, source_target_pairs={{0,1},{2,3},{4,5},{6,7},{8,9},{10,11},{12,13},{14,15},{16,17},{18,... | collective-permute-start | bytes 12296 | tf_op jit(solution)/shard_map/ppermute | solution.py:18
  86.0 11.0 %all-to-all-start.2 = ((f32[16,1,1024]{2,1,0:T(1,128)}), f32[16,1,1024]{2,1,0:T(1,128)S(1)}, u32[]{:S(2)}, u32[]{:S(2)}) async-start(f32[16,1,1024]{2,1,0:T(1,128)} %reshape.140), calls=%async_computation.2 | async-start | bytes 131072 | tf_op jit(solution)/shard_map/all_to_all | solution.py:87
  105.6 24.0 %copy-start = (f32[4,2,1,8,512]{4,3,2,1,0:T(8,128)S(1)}, f32[4,2,1,8,512]{4,3,2,1,0:T(8,128)}, u32[]{:S(2)}) copy-start(f32[4,2,1,8,512]{4,3,2,1,0:T(8,128)} %param.3) | copy-start | bytes 393220
  119.8 7.8 %collective-permute-start.6 = (f32[2,8,512]{2,1,0:T(8,128)S(1)}, f32[2,8,512]{2,1,0:T(8,128)S(1)}, u32[]{:S(2)}, u32[]{:S(2)}) collective-permute-start(f32[2,8,512]{2,1,0:T(8,128)S(1)} %reshape_squeeze.15), channel_id=1, source_target_pairs={{0,2},{2,4},{4,6},{6,8},{8,10},{10,12},{12,14},{14,16},{16,18},{18... | collective-permute-start | bytes 98312 | tf_op jit(solution)/shard_map/ppermute | solution.py:27
  122.4 4.4 %collective-permute-start.7 = (f32[1,1,512]{2,1,0:T(1,128)S(1)}, f32[1,1,512]{2,1,0:T(1,128)S(1)}, u32[]{:S(2)}, u32[]{:S(2)}) collective-permute-start(f32[1,1,512]{2,1,0:T(1,128)S(1)} %get-tuple-element.29), channel_id=1, source_target_pairs={{1,0},{3,2},{5,4},{7,6},{9,8},{11,10},{13,12},{15,14},{17,16},{19,... | collective-permute-start | bytes 6152 | tf_op jit(solution)/shard_map/ppermute | solution.py:19
  123.7 3.8 %collective-permute-start.8 = (f32[1,1,512]{2,1,0:T(1,128)S(1)}, f32[1,1,512]{2,1,0:T(1,128)S(1)}, u32[]{:S(2)}, u32[]{:S(2)}) collective-permute-start(f32[1,1,512]{2,1,0:T(1,128)S(1)} %get-tuple-element.30), channel_id=1, source_target_pairs={{0,1},{2,3},{4,5},{6,7},{8,9},{10,11},{12,13},{14,15},{16,17},{18,... | collective-permute-start | bytes 6152 | tf_op jit(solution)/shard_map/ppermute | solution.py:18
where the time goes:
time: 170 us; the launch traced here: 169 us
  blocking collectives  64.5 us (38%)
  local copies, waits for them, and re-layouts  33.7 us (20%)
  starting transfers between devices  27 us (16%)
  other arithmetic  23.6 us (14%)
  waiting for transfers between devices  17.7 us (10%)
  between operations  2.06 us (1%)
    psum x1, blocking collectives, on_device(): gram = lax.psum(local_terms, ('tm', 'rows'))  39 us
    unnamed x10, local copies, waits for them, and re-layouts  22.8 us
    unnamed x1, other arithmetic  19.4 us
    all_to_all x1, blocking collectives, on_device(): lax.all_to_all(scaled.reshape(1, 2, cells), 'tm', split_axis=2, concat_ax...  15.5 us
    ppermute x4, starting transfers between devices, padded_2(): before = lax.ppermute(last, axis, up)  12.3 us
    all_to_all x1, blocking collectives, on_device(): lax.all_to_all(history, 'tm', split_axis=0, concat_axis=2, tiled=True)  9.98 us
    all_to_all x1, waiting for transfers between devices, on_device(): lax.all_to_all(yhat.reshape(1, 2, 2, cells), 'tm', split_axis=3, concat_a...  7.49 us
    all_to_all x1, waiting for transfers between devices, on_device(): lax.all_to_all(stacked, 'tm', split_axis=0, concat_axis=3, tiled=True)  7.25 us
  transfers between devices with their start and end apart: 11, of which 6 were waited for; matrix products, arithmetic and copies ran while one was open for 0% of the time, Pallas kernels for 0%

commit v1 on v0

--- a/solution.py
+++ b/solution.py
@@ -106,7 +106,7 @@
     count = 2.0 * steps * rows_dev * lax.axis_size("rows") * cols
     squares = jnp.sum(image * image) / count
     local_terms = jnp.concatenate([inner, squares[None]])
-    gram = lax.psum(local_terms, ("tm", "rows"))
+    gram = lax.psum(lax.psum(local_terms, "rows"), "tm")
     return (precond[:, None], image[:, None], gram)
 
 

time: 170 us -> 172 us (1.012)
  blocking collectives: 64.5 us -> 66.4 us
    psum x1 -> x2, blocking collectives: 39 us -> 40.9 us  [on_device(): gram = lax.psum(lax.psum(local_terms, 'rows'), 'tm')]
where the time goes in v1:
time: 172 us; the launch traced here: 171 us
  blocking collectives  66.4 us (39%)
  local copies, waits for them, and re-layouts  33.7 us (20%)
  starting transfers between devices  27 us (16%)
  other arithmetic  23.6 us (14%)
  waiting for transfers between devices  17.7 us (10%)
  between operations  2.02 us (1%)
    psum x2, blocking collectives, on_device(): gram = lax.psum(lax.psum(local_terms, 'rows'), 'tm')  40.9 us
    unnamed x10, local copies, waits for them, and re-layouts  22.8 us
    unnamed x1, other arithmetic  19.4 us
    all_to_all x1, blocking collectives, on_device(): lax.all_to_all(scaled.reshape(1, 2, cells), 'tm', split_axis=2, concat_ax...  15.5 us
    ppermute x4, starting transfers between devices, padded_2(): before = lax.ppermute(last, axis, up)  12.3 us
    all_to_all x1, blocking collectives, on_device(): lax.all_to_all(history, 'tm', split_axis=0, concat_axis=2, tiled=True)  9.98 us
    all_to_all x1, waiting for transfers between devices, on_device(): lax.all_to_all(yhat.reshape(1, 2, 2, cells), 'tm', split_axis=3, concat_a...  7.49 us
    all_to_all x1, waiting for transfers between devices, on_device(): lax.all_to_all(stacked, 'tm', split_axis=0, concat_axis=3, tiled=True)  7.25 us
  transfers between devices with their start and end apart: 11, of which 6 were waited for; matrix products, arithmetic and copies ran while one was open for 0% of the time, Pallas kernels for 0%

profile of v1, /device:TPU:0, one launch (start us, length us, event | category | flops | bytes accessed | tf_op | source)
XLA Modules:
  0.0 171.3 jit_solution(7038172421289063082)
XLA Ops:
  0.7 0.8 broadcast_multiply_fusion
  1.4 0.6 copy.44
  2.1 0.5 broadcast.139
  2.6 19.4 %reduce.4 = f32[4096,2]{1,0:T(8,128)} reduce(f32[4096,1,2]{2,1,0:T(1,128)S(1)} %bitcast.83, f32[]{:T(128)} %broadcast.139), dimensions={1}, to_apply=%bitcast.65.reduce_sub_computation | reduce | bytes 65540
  22.0 3.0 %reshape.138 = f32[16,1,512]{2,1,0:T(1,128)S(1)} reshape(f32[4096,2]{1,0:T(8,128)} %reduce.4) | data formatting | bytes 65536
  25.0 15.5 %all_to_all.63 = f32[16,1,512]{2,1,0:T(1,128)S(1)} all-to-all(f32[16,1,512]{2,1,0:T(1,128)S(1)} %reshape.138), channel_id=1, replica_groups=mesh['tm'=16,'rows'=2] {'tm'}, dimensions={0} | all-to-all | bytes 65536 | tf_op jit(solution)/shard_map/all_to_all | solution.py:61
  40.6 0.7 reduce.5
  41.3 3.4 %reshape.139 = f32[4096,1,2]{2,1,0:T(1,128)S(1)} reshape(f32[16,512]{1,0:T(8,128)S(1)} %reduce.5) | data formatting | bytes 65536
  44.7 0.6 copy.45
  45.3 0.2 convolution_bitcast_fusion
  45.5 0.2 convolution_negate_fusion
  45.8 0.7 copy.48
  46.5 3.5 %all-to-all-start.1 = ((f32[16,2,2,256]{3,2,1,0:T(2,128)}), f32[16,2,2,256]{3,2,1,0:T(2,128)S(1)}, u32[]{:S(2)}, u32[]{:S(2)}) async-start(f32[16,2,2,256]{3,2,1,0:T(2,128)} %copy.48), calls=%async_computation.1 | async-start | bytes 131072 | tf_op jit(solution)/shard_map/all_to_all | solution.py:68
  50.3 7.2 %all-to-all-done.1 = f32[16,2,2,256]{3,2,1,0:T(2,128)S(1)} async-done(((f32[16,2,2,256]{3,2,1,0:T(2,128)}), f32[16,2,2,256]{3,2,1,0:T(2,128)S(1)}, u32[]{:S(2)}, u32[]{:S(2)}) %all-to-all-start.1) | async-done | bytes 65568 | tf_op jit(solution)/shard_map/all_to_all | solution.py:68
  57.6 1.3 collective-permute-start
  58.9 3.0 %collective-permute-start.1 = (f32[2,1,512]{2,1,0:T(1,128)S(1)}, f32[2,1,512]{2,1,0:T(1,128)S(1)}, u32[]{:S(2)}, u32[]{:S(2)}) collective-permute-start(f32[2,1,512]{2,1,0:T(1,128)S(1)} %get-tuple-element.26), channel_id=1, source_target_pairs={{0,1},{2,3},{4,5},{6,7},{8,9},{10,11},{12,13},{14,15},{16,17},{18,... | collective-permute-start | bytes 12296 | tf_op jit(solution)/shard_map/ppermute | solution.py:18
  62.0 0.8 collective-permute-done.1
  62.8 0.1 fusion.5
  62.9 1.3 collective-permute-start.2
  64.2 3.0 %collective-permute-start.3 = (f32[2,1,512]{2,1,0:T(1,128)S(1)}, f32[2,1,512]{2,1,0:T(1,128)S(1)}, u32[]{:S(2)}, u32[]{:S(2)}) collective-permute-start(f32[2,1,512]{2,1,0:T(1,128)S(1)} %get-tuple-element.22), channel_id=1, source_target_pairs={{0,1},{2,3},{4,5},{6,7},{8,9},{10,11},{12,13},{14,15},{16,17},{18,... | collective-permute-start | bytes 12296 | tf_op jit(solution)/shard_map/ppermute | solution.py:18
  67.2 0.8 collective-permute-done.3
  68.0 0.1 fusion.9
  68.1 1.3 collective-permute-start.4
  69.4 3.2 %collective-permute-start.5 = (f32[2,1,512]{2,1,0:T(1,128)S(1)}, f32[2,1,512]{2,1,0:T(1,128)S(1)}, u32[]{:S(2)}, u32[]{:S(2)}) collective-permute-start(f32[2,1,512]{2,1,0:T(1,128)S(1)} %get-tuple-element.18), channel_id=1, source_target_pairs={{0,1},{2,3},{4,5},{6,7},{8,9},{10,11},{12,13},{14,15},{16,17},{18,... | collective-permute-start | bytes 12296 | tf_op jit(solution)/shard_map/ppermute | solution.py:18
  72.7 0.6 collective-permute-done.5
  73.3 0.1 fusion.13
  73.5 4.4 %copy.51 = f32[1,2,2,4096]{2,1,0,3:T(2,128)} copy(f32[1,2,2,4096]{3,1,2,0:T(2,128)S(1)} %pad_maximum_fusion.1) | data formatting | bytes 131072 | tf_op jit(solution)/shard_map/stack | solution.py:86
  77.9 8.1 %reshape.140 = f32[16,1,1024]{2,1,0:T(1,128)} reshape(f32[4096,1,2,2]{3,2,1,0:T(2,128)} %bitcast.81) | data formatting | bytes 131072
  86.0 3.5 %all-to-all-start.2 = ((f32[16,1,1024]{2,1,0:T(1,128)}), f32[16,1,1024]{2,1,0:T(1,128)S(1)}, u32[]{:S(2)}, u32[]{:S(2)}) async-start(f32[16,1,1024]{2,1,0:T(1,128)} %reshape.140), calls=%async_computation.2 | async-start | bytes 131072 | tf_op jit(solution)/shard_map/all_to_all | solution.py:87
  89.5 7.5 %all-to-all-done.2 = f32[16,1,1024]{2,1,0:T(1,128)S(1)} async-done(((f32[16,1,1024]{2,1,0:T(1,128)}), f32[16,1,1024]{2,1,0:T(1,128)S(1)}, u32[]{:S(2)}, u32[]{:S(2)}) %all-to-all-start.2) | async-done | bytes 65568 | tf_op jit(solution)/shard_map/all_to_all | solution.py:87
  97.0 0.8 reduce.6
  97.8 7.7 %reshape.141 = f32[4096,1,2,2]{3,2,1,0:T(2,128)} reshape(f32[16,1024]{1,0:T(8,128)S(1)} %reduce.6) | data formatting | bytes 131072
  105.6 3.6 %copy.57 = f32[1,2,2,16,256]{4,3,2,1,0:T(8,128)S(1)} copy(f32[1,2,2,16,256]{2,1,4,3,0:T(2,128)} %bitcast.82) | data formatting | bytes 131072 | tf_op jit(solution)/shard_map/all_to_all | solution.py:87
  109.2 0.2 fusion.42
  109.5 0.2 fusion
  109.7 10.0 %all_to_all.64 = f32[16,2,256]{2,1,0:T(2,128)S(1)} all-to-all(f32[16,2,256]{2,1,0:T(2,128)S(1)} %reshape.134), channel_id=1, replica_groups=mesh['tm'=16,'rows'=2] {'tm'}, dimensions={0} | all-to-all | bytes 65536 | tf_op jit(solution)/shard_map/all_to_all | solution.py:97
  119.7 0.1 slice_reduce_fusion
  119.8 2.6 %collective-permute-start.6 = (f32[2,8,512]{2,1,0:T(8,128)S(1)}, f32[2,8,512]{2,1,0:T(8,128)S(1)}, u32[]{:S(2)}, u32[]{:S(2)}) collective-permute-start(f32[2,8,512]{2,1,0:T(8,128)S(1)} %reshape_squeeze.15), channel_id=1, source_target_pairs={{0,2},{2,4},{4,6},{6,8},{8,10},{10,12},{12,14},{14,16},{16,18},{18... | collective-permute-start | bytes 98312 | tf_op jit(solution)/shard_map/ppermute | solution.py:27
  122.5 1.3 collective-permute-start.7
  123.8 3.0 %collective-permute-start.8 = (f32[1,1,512]{2,1,0:T(1,128)S(1)}, f32[1,1,512]{2,1,0:T(1,128)S(1)}, u32[]{:S(2)}, u32[]{:S(2)}) collective-permute-start(f32[1,1,512]{2,1,0:T(1,128)S(1)} %get-tuple-element.30), channel_id=1, source_target_pairs={{0,1},{2,3},{4,5},{6,7},{8,9},{10,11},{12,13},{14,15},{16,17},{18,... | collective-permute-start | bytes 6152 | tf_op jit(solution)/shard_map/ppermute | solution.py:18
  126.8 0.8 collective-permute-done.8
  127.6 0.1 fusion.26
  127.7 1.2 pad_maximum_fusion.18
  129.6 0.1 fusion.1
  129.7 0.1 pad_maximum_fusion.21
  129.8 2.5 %psum.14 = f32[5]{0:T(128)S(1)} all-reduce(f32[5]{0:T(128)S(1)} %pad_maximum_fusion.21), channel_id=1, replica_groups=mesh['tm'=16,'rows'=2] {'rows'}, use_global_device_ids=true, to_apply=%region_2.3 | all-reduce | flops 5 | bytes 40 | tf_op jit(solution)/shard_map/psum | solution.py:109
  132.2 0.6 broadcast_in_dim_reshape_squeeze.3
  132.8 38.4 %psum.15 = f32[5]{0:T(128)} all-reduce(f32[5]{0:T(128)S(1)} %psum.14), channel_id=1, replica_groups=mesh['tm'=16,'rows'=2] {'tm'}, use_global_device_ids=true, to_apply=%region_3.4 | all-reduce | flops 5 | bytes 40 | tf_op jit(solution)/shard_map/psum | solution.py:109
  (43 shorter events, 0.5 us)
Async XLA Ops:
  46.5 11.0 %all-to-all-start.1 = ((f32[16,2,2,256]{3,2,1,0:T(2,128)}), f32[16,2,2,256]{3,2,1,0:T(2,128)S(1)}, u32[]{:S(2)}, u32[]{:S(2)}) async-start(f32[16,2,2,256]{3,2,1,0:T(2,128)} %copy.48), calls=%async_computation.1 | async-start | bytes 131072 | tf_op jit(solution)/shard_map/all_to_all | solution.py:68
  57.6 4.3 %collective-permute-start = (f32[2,1,512]{2,1,0:T(1,128)S(1)}, f32[2,1,512]{2,1,0:T(1,128)S(1)}, u32[]{:S(2)}, u32[]{:S(2)}) collective-permute-start(f32[2,1,512]{2,1,0:T(1,128)S(1)} %get-tuple-element.25), channel_id=1, source_target_pairs={{1,0},{3,2},{5,4},{7,6},{9,8},{11,10},{13,12},{15,14},{17,16},{19,... | collective-permute-start | bytes 12296 | tf_op jit(solution)/shard_map/ppermute | solution.py:19
  58.9 3.8 %collective-permute-start.1 = (f32[2,1,512]{2,1,0:T(1,128)S(1)}, f32[2,1,512]{2,1,0:T(1,128)S(1)}, u32[]{:S(2)}, u32[]{:S(2)}) collective-permute-start(f32[2,1,512]{2,1,0:T(1,128)S(1)} %get-tuple-element.26), channel_id=1, source_target_pairs={{0,1},{2,3},{4,5},{6,7},{8,9},{10,11},{12,13},{14,15},{16,17},{18,... | collective-permute-start | bytes 12296 | tf_op jit(solution)/shard_map/ppermute | solution.py:18
  62.9 4.3 %collective-permute-start.2 = (f32[2,1,512]{2,1,0:T(1,128)S(1)}, f32[2,1,512]{2,1,0:T(1,128)S(1)}, u32[]{:S(2)}, u32[]{:S(2)}) collective-permute-start(f32[2,1,512]{2,1,0:T(1,128)S(1)} %get-tuple-element.21), channel_id=1, source_target_pairs={{1,0},{3,2},{5,4},{7,6},{9,8},{11,10},{13,12},{15,14},{17,16},{19,... | collective-permute-start | bytes 12296 | tf_op jit(solution)/shard_map/ppermute | solution.py:19
  64.2 3.8 %collective-permute-start.3 = (f32[2,1,512]{2,1,0:T(1,128)S(1)}, f32[2,1,512]{2,1,0:T(1,128)S(1)}, u32[]{:S(2)}, u32[]{:S(2)}) collective-permute-start(f32[2,1,512]{2,1,0:T(1,128)S(1)} %get-tuple-element.22), channel_id=1, source_target_pairs={{0,1},{2,3},{4,5},{6,7},{8,9},{10,11},{12,13},{14,15},{16,17},{18,... | collective-permute-start | bytes 12296 | tf_op jit(solution)/shard_map/ppermute | solution.py:18
  68.1 4.5 %collective-permute-start.4 = (f32[2,1,512]{2,1,0:T(1,128)S(1)}, f32[2,1,512]{2,1,0:T(1,128)S(1)}, u32[]{:S(2)}, u32[]{:S(2)}) collective-permute-start(f32[2,1,512]{2,1,0:T(1,128)S(1)} %get-tuple-element.17), channel_id=1, source_target_pairs={{1,0},{3,2},{5,4},{7,6},{9,8},{11,10},{13,12},{15,14},{17,16},{19,... | collective-permute-start | bytes 12296 | tf_op jit(solution)/shard_map/ppermute | solution.py:19
  69.4 3.8 %collective-permute-start.5 = (f32[2,1,512]{2,1,0:T(1,128)S(1)}, f32[2,1,512]{2,1,0:T(1,128)S(1)}, u32[]{:S(2)}, u32[]{:S(2)}) collective-permute-start(f32[2,1,512]{2,1,0:T(1,128)S(1)} %get-tuple-element.18), channel_id=1, source_target_pairs={{0,1},{2,3},{4,5},{6,7},{8,9},{10,11},{12,13},{14,15},{16,17},{18,... | collective-permute-start | bytes 12296 | tf_op jit(solution)/shard_map/ppermute | solution.py:18
  86.0 11.0 %all-to-all-start.2 = ((f32[16,1,1024]{2,1,0:T(1,128)}), f32[16,1,1024]{2,1,0:T(1,128)S(1)}, u32[]{:S(2)}, u32[]{:S(2)}) async-start(f32[16,1,1024]{2,1,0:T(1,128)} %reshape.140), calls=%async_computation.2 | async-start | bytes 131072 | tf_op jit(solution)/shard_map/all_to_all | solution.py:87
  105.6 24.0 %copy-start = (f32[4,2,1,8,512]{4,3,2,1,0:T(8,128)S(1)}, f32[4,2,1,8,512]{4,3,2,1,0:T(8,128)}, u32[]{:S(2)}) copy-start(f32[4,2,1,8,512]{4,3,2,1,0:T(8,128)} %param.3) | copy-start | bytes 393220
  119.8 7.8 %collective-permute-start.6 = (f32[2,8,512]{2,1,0:T(8,128)S(1)}, f32[2,8,512]{2,1,0:T(8,128)S(1)}, u32[]{:S(2)}, u32[]{:S(2)}) collective-permute-start(f32[2,8,512]{2,1,0:T(8,128)S(1)} %reshape_squeeze.15), channel_id=1, source_target_pairs={{0,2},{2,4},{4,6},{6,8},{8,10},{10,12},{12,14},{14,16},{16,18},{18... | collective-permute-start | bytes 98312 | tf_op jit(solution)/shard_map/ppermute | solution.py:27
  122.5 4.4 %collective-permute-start.7 = (f32[1,1,512]{2,1,0:T(1,128)S(1)}, f32[1,1,512]{2,1,0:T(1,128)S(1)}, u32[]{:S(2)}, u32[]{:S(2)}) collective-permute-start(f32[1,1,512]{2,1,0:T(1,128)S(1)} %get-tuple-element.29), channel_id=1, source_target_pairs={{1,0},{3,2},{5,4},{7,6},{9,8},{11,10},{13,12},{15,14},{17,16},{19,... | collective-permute-start | bytes 6152 | tf_op jit(solution)/shard_map/ppermute | solution.py:19
  123.8 3.8 %collective-permute-start.8 = (f32[1,1,512]{2,1,0:T(1,128)S(1)}, f32[1,1,512]{2,1,0:T(1,128)S(1)}, u32[]{:S(2)}, u32[]{:S(2)}) collective-permute-start(f32[1,1,512]{2,1,0:T(1,128)S(1)} %get-tuple-element.30), channel_id=1, source_target_pairs={{0,1},{2,3},{4,5},{6,7},{8,9},{10,11},{12,13},{14,15},{16,17},{18,... | collective-permute-start | bytes 6152 | tf_op jit(solution)/shard_map/ppermute | solution.py:18
